TPU v7x, 32 devices: a whole 2x2x4 slice. The times are simulated.
32 devices in a mesh: gx: 4 (over z), gy: 4 (over y, x), gz: 2 (over core).
Axes of the slice: x: 2, y: 2, z: 4, core: 2. Of those that a mesh axis runs over, the one named last changes fastest.
Arguments:
- right_side: float32 [4, 96, 96, 48], P(None, 'gx', 'gy', 'gz'), may hold values from -6 to 6
- iterate: float32 [4, 96, 96, 48], P(None, 'gx', 'gy', 'gz'), may hold values from -6 to 6
- coefficient: float32 [96, 96, 48], P('gx', 'gy', 'gz'), may hold values from 0.1 to 2
- ordering: int32 [4, 4, 2, 216], P('gx', 'gy', 'gz'), may hold values from 0 to 215, as said below
- leaf_inverse: float32 [4, 4, 2, 125, 125], P('gx', 'gy', 'gz'), may hold values from -2 to 3
- leaf_first: float32 [4, 4, 2, 125, 50], P('gx', 'gy', 'gz'), may hold values from -0.5 to 0.5
- leaf_second: float32 [4, 4, 2, 125, 60], P('gx', 'gy', 'gz'), may hold values from -0.5 to 0.5
- leaf_top: float32 [4, 4, 2, 125, 72], P('gx', 'gy', 'gz'), may hold values from -0.5 to 0.5
- first_inverse: float32 [4, 4, 50, 50], P('gx', 'gy', 'gz'), may hold values from -2 to 3
- first_second: float32 [4, 4, 2, 25, 60], P('gx', 'gy', 'gz'), may hold values from -1.25 to 1.25
- first_top: float32 [4, 4, 2, 25, 72], P('gx', 'gy', 'gz'), may hold values from -1.25 to 1.25
- second_inverse: float32 [4, 240, 240], P('gx', ('gy', 'gz')), may hold values from -2 to 3
- second_top: float32 [4, 4, 2, 30, 72], P('gx', 'gy', 'gz'), may hold values from -1 to 1
- top_inverse: float32 [1152, 1152], P(('gx', 'gy', 'gz')), may hold values from -2 to 3
Outputs:
- correction: float32 [4, 96, 96, 48], P(None, 'gx', 'gy', 'gz')
Inputs may be any that keep to these rules, and one draw needn't show every extreme that they name: `ordering`: each device's row names each of its 216 coarse cells once (cell x 6^2 + y * 6 + z): first the 125 cells with x, y and z all below 5, then the 25 cells with z = 5 and x, y below it, then the 30 cells with y = 5 and x below it, then the 36 cells with x = 5, each group in any order.
All inputs are finite; a program needn't handle non-finite values.
Results may differ from a plain program's by a relative error of at most 0.0003.
Values sent between devices are 32-bit elements; how exact they have to be, the bound alone decides.
A program may use at most 64 MiB of HBM per device.

v0:
```python
import jax
import jax.numpy as jnp
from jax import lax
from jax.sharding import PartitionSpec as P

precise = lax.Precision.HIGHEST


def shifted(shard, axis, by):
    peers = lax.axis_size(axis)
    pairs = [(i, i + by) for i in range(peers) if 0 <= i + by < peers]
    return lax.ppermute(shard, axis, pairs)


def with_halo(cells, sides, width):
    for axis, dim in sides:
        count = lax.axis_size(axis)
        ends = count - 1
        head = lax.slice_in_dim(cells, 0, width, axis=dim)
        tail = lax.slice_in_dim(cells, cells.shape[dim] - width, cells.shape[dim], axis=dim)
        cells = jnp.concatenate(
            [
                lax.ppermute(tail, axis, [(i, (i + 1) % count) for i in range(ends)]),
                cells,
                lax.ppermute(head, axis, [((i + 1) % count, i) for i in range(ends)]),
            ],
            axis=dim,
        )
    return cells


def product(operand, matrix):
    return jnp.dot(operand, matrix, precision=precise, preferred_element_type=jnp.float32)


def product_back(operand, matrix):
    return lax.dot_general(
        operand,
        matrix,
        (((1,), (1,)), ((), ())),
        precision=precise,
        preferred_element_type=jnp.float32,
    )


def weigh(extended, dimension):
    length = extended.shape[dimension] - 1
    previous = lax.slice_in_dim(extended, 0, length, 2, dimension)
    centre = lax.slice_in_dim(extended, 1, length + 1, 2, dimension)
    following = lax.slice_in_dim(extended, 2, length + 1, 2, dimension)
    return 0.25 * previous + 0.5 * centre + 0.25 * following


def spread(extended, dimension):
    length = extended.shape[dimension] - 1
    current = lax.slice_in_dim(extended, 0, length, 1, dimension)
    following = lax.slice_in_dim(extended, 1, length + 1, 1, dimension)
    paired = jnp.stack([current, 0.5 * (current + following)], axis=dimension + 1)
    new_shape = list(current.shape)
    new_shape[dimension] = 2 * length
    return paired.reshape(new_shape)


def lower_rims(values):
    boundary = shifted(values[:, -1:], "gx", 1)
    values = jnp.concatenate([boundary, values], axis=1)
    boundary = shifted(values[:, :, -1:], "gy", 1)
    values = jnp.concatenate([boundary, values], axis=2)
    boundary = shifted(values[:, :, :, -1:], "gz", 1)
    return jnp.concatenate([boundary, values], axis=3)


def upper_rims(values):
    boundary = shifted(values[:, :1], "gx", -1)
    values = jnp.concatenate([values, boundary], axis=1)
    boundary = shifted(values[:, :, :1], "gy", -1)
    values = jnp.concatenate([values, boundary], axis=2)
    boundary = shifted(values[:, :, :, :1], "gz", -1)
    return jnp.concatenate([values, boundary], axis=3)


def restrict(values):
    extended = lower_rims(values)
    for dimension in (1, 2, 3):
        extended = weigh(extended, dimension)
    return extended


def prolong(values):
    extended = upper_rims(values)
    for dimension in (1, 2, 3):
        extended = spread(extended, dimension)
    return extended


def residual_of(right_side, iterate, coefficient):
    padded = with_halo(iterate, (("gx", 1), ("gy", 2), ("gz", 3)), 1)
    beside = padded[:, 2:, 1:-1, 1:-1] + padded[:, :-2, 1:-1, 1:-1]
    beside = beside + padded[:, 1:-1, 2:, 1:-1] + padded[:, 1:-1, :-2, 1:-1]
    beside = beside + padded[:, 1:-1, 1:-1, 2:] + padded[:, 1:-1, 1:-1, :-2]
    return right_side - ((6.0 + coefficient) * iterate - beside)


def per_device(
    right_side,
    iterate,
    coefficient,
    ordering,
    leaf_inverse,
    leaf_first,
    leaf_second,
    leaf_top,
    first_inverse,
    first_second,
    first_top,
    second_inverse,
    second_top,
    top_inverse,
):
    rhs_count = right_side.shape[0]
    leaf_size = leaf_inverse.shape[-1]
    first_size = first_second.shape[3]
    second_size = second_top.shape[3]
    top_size = top_inverse.shape[0]
    first_rows = first_inverse[0, 0]
    second_rows = second_inverse[0]
    first_start = lax.axis_index("gz") * first_size
    first_full = lax.all_gather(first_rows, "gz", axis=0, tiled=True)
    first_columns = lax.dynamic_slice_in_dim(first_full, first_start, first_size, 1)
    coarse = restrict(restrict(residual_of(right_side, iterate, coefficient)))
    coarse_side = coarse.shape[1]
    flattened = coarse.reshape(rhs_count, coarse_side**3)
    order_row = ordering.reshape(-1)
    chosen = jnp.take(flattened, order_row, axis=1)
    first_end = leaf_size + first_size
    second_end = first_end + second_size
    leaf_rhs = chosen[:, :leaf_size]
    first_rhs = chosen[:, leaf_size:first_end]
    second_rhs = chosen[:, first_end:second_end]
    top_rhs = chosen[:, second_end:]
    leaf_block = leaf_inverse[0, 0, 0]
    to_first = leaf_first[0, 0, 0]
    to_second = leaf_second[0, 0, 0]
    to_top = leaf_top[0, 0, 0]
    first_to_second = first_second[0, 0, 0]
    first_to_top = first_top[0, 0, 0]
    second_to_top = second_top[0, 0, 0]
    leaf_solved = product(leaf_rhs, leaf_block)
    toward = product(leaf_solved, to_first)
    arrived = shifted(toward[:, first_size:], "gz", -1)
    first_target = first_rhs - toward[:, :first_size] - arrived
    target_whole = lax.all_gather(first_target, "gz", axis=1, tiled=True)
    first_own = product(target_whole, first_columns)
    toward = product(leaf_solved, to_second) + product(first_own, first_to_second)
    arrived = shifted(toward[:, second_size:], "gy", -1)
    second_target = second_rhs - toward[:, :second_size] - arrived
    second_own = lax.psum_scatter(
        product(second_target, second_rows), ("gy", "gz"), scatter_dimension=1, tiled=True
    )
    toward = (
        product(leaf_solved, to_top)
        + product(first_own, first_to_top)
        + product(second_own, second_to_top)
    )
    arrived = shifted(toward[:, top_size:], "gx", -1)
    top_target = top_rhs - toward[:, :top_size] - arrived
    top_own = lax.psum_scatter(
        product(top_target, top_inverse), ("gx", "gy", "gz"), scatter_dimension=1, tiled=True
    )
    top_whole = lax.all_gather(top_own, ("gx", "gy", "gz"), axis=1, tiled=True)
    top_back = product_back(top_whole, top_inverse)
    top_lower = shifted(top_back, "gx", 1)
    top_pair = jnp.concatenate([top_back, top_lower], axis=1)
    second_gap = second_own - product_back(top_pair, second_to_top)
    second_whole = lax.all_gather(second_gap, ("gy", "gz"), axis=1, tiled=True)
    second_back = product_back(second_whole, second_rows)
    second_lower = shifted(second_back, "gy", 1)
    second_pair = jnp.concatenate([second_back, second_lower], axis=1)
    first_gap = (
        first_own
        - product_back(second_pair, first_to_second)
        - product_back(top_pair, first_to_top)
    )
    first_whole = lax.all_gather(first_gap, "gz", axis=1, tiled=True)
    first_back = product_back(first_whole, first_rows)
    first_lower = shifted(first_back, "gz", 1)
    first_pair = jnp.concatenate([first_back, first_lower], axis=1)
    leaf_gap = (
        leaf_solved - product_back(first_pair, to_first) - product_back(second_pair, to_second)
    )
    leaf_gap = leaf_gap - product_back(top_pair, to_top)
    leaf_back = product_back(leaf_gap, leaf_block)
    ordered = jnp.concatenate([leaf_back, first_back, second_back, top_back], axis=1)
    coarse_cells = jnp.zeros_like(ordered).at[:, order_row].set(ordered)
    coarse_grid = coarse_cells.reshape(rhs_count, coarse_side, coarse_side, coarse_side)
    return prolong(prolong(coarse_grid))


def solution(mesh):
    return jax.shard_map(
        per_device,
        mesh=mesh,
        in_specs=(
            P(None, "gx", "gy", "gz"),
            P(None, "gx", "gy", "gz"),
            P("gx", "gy", "gz"),
            P("gx", "gy", "gz", None),
            P("gx", "gy", "gz", None, None),
            P("gx", "gy", "gz", None, None),
            P("gx", "gy", "gz", None, None),
            P("gx", "gy", "gz", None, None),
            P("gx", "gy", "gz", None),
            P("gx", "gy", "gz", None, None),
            P("gx", "gy", "gz", None, None),
            P("gx", ("gy", "gz"), None),
            P("gx", "gy", "gz", None, None),
            P(("gx", "gy", "gz"), None),
        ),
        out_specs=P(None, "gx", "gy", "gz"),
        check_vma=False,
    )
```

profile of v0, /device:TPU:0, one launch (start us, length us, event | category | flops | bytes accessed | tf_op | source)
XLA Modules:
  0.0 293.6 jit_solution(13946960478446539935)
XLA Ops:
  0.9 1.3 collective-permute-start
  2.2 5.6 %collective-permute-start.1 = (f32[4,1,24,24]{3,2,1,0:T(8,128)S(1)}, f32[4,1,24,24]{3,2,1,0:T(8,128)S(1)}, u32[]{:S(2)}, u32[]{:S(2)}) collective-permute-start(f32[4,1,24,24]{3,2,1,0:T(8,128)S(1)} %get-tuple-element.9), channel_id=1, source_target_pairs={{0,8},{8,16},{16,24},{1,9},{9,17},{17,25},{2,10},{10,18},{18,26},{... | collective-permute-start | bytes 27656 | tf_op jit(solution)/shard_map/ppermute | solution.py:23
  7.8 1.6 copy.139
  10.1 1.7 copy.142
  11.7 1.0 pad_maximum_fusion.36
  12.8 1.3 collective-permute-start.2
  14.1 4.7 %collective-permute-start.3 = (f32[4,26,1,24]{1,3,2,0:T(8,128)S(1)}, f32[4,26,1,24]{1,3,2,0:T(8,128)S(1)}, u32[]{:S(2)}, u32[]{:S(2)}) collective-permute-start(f32[4,26,1,24]{1,3,2,0:T(8,128)S(1)} %get-tuple-element.7), channel_id=1, source_target_pairs={{0,2},{2,4},{4,6},{1,3},{3,5},{5,7},{8,10},{10,12},{12,14},{9,11},... | collective-permute-start | bytes 29960 | tf_op jit(solution)/shard_map/ppermute | solution.py:23
  18.8 1.7 collective-permute-done.3
  21.1 1.3 collective-permute-start.4
  22.5 3.0 %collective-permute-start.5 = (f32[4,26,26,1]{2,1,3,0:T(8,128)S(1)}, f32[4,26,26,1]{2,1,3,0:T(8,128)S(1)}, u32[]{:S(2)}, u32[]{:S(2)}) collective-permute-start(f32[4,26,26,1]{2,1,3,0:T(8,128)S(1)} %copy.149), channel_id=1, source_target_pairs={{0,1},{2,3},{4,5},{6,7},{8,9},{10,11},{12,13},{14,15},{16,17},{18,... | collective-permute-start | bytes 32456 | tf_op jit(solution)/shard_map/ppermute | solution.py:23
  25.6 2.7 copy.151
  28.7 9.4 %fusion.2 = f32[4,24,24,24]{1,3,2,0:T(8,128)S(1)} fusion(f32[4,24,24,24]{1,3,2,0:T(8,128)} %copy.151, f32[4,26,26,1]{1,3,2,0:T(1,128)S(1)} %copy.150, f32[4,26,1,24]{1,3,2,0:T(8,128)S(1)} %collective-permute-done.2, f32[4,26,1,24]{1,3,2,0:T(8,128)S(1)} %collective-permute-done.3, f32[4,1,24,24]{1,3,2,0:T(8,128)} %copy-done.1, ...), kind=kLoop, calls=%fused_computation.7 | loop fusion | flops 1437696 | bytes 778880 | tf_op jit(solution)/shard_map/sub | solution.py:101
  39.0 3.9 %collective-permute-start.6 = (f32[4,1,24,24]{3,2,1,0:T(8,128)S(1)}, f32[4,1,24,24]{3,2,1,0:T(8,128)S(1)}, u32[]{:S(2)}, u32[]{:S(2)}) collective-permute-start(f32[4,1,24,24]{3,2,1,0:T(8,128)S(1)} %copy.152), channel_id=1, source_target_pairs={{0,8},{8,16},{16,24},{1,9},{9,17},{17,25},{2,10},{10,18},{18,26},{... | collective-permute-start | bytes 27656 | tf_op jit(solution)/shard_map/ppermute | solution.py:12
  43.0 1.7 collective-permute-done.6
  45.4 4.5 %collective-permute-start.7 = (f32[4,25,1,24]{1,3,2,0:T(8,128)S(1)}, f32[4,25,1,24]{1,3,2,0:T(8,128)S(1)}, u32[]{:S(2)}, u32[]{:S(2)}) collective-permute-start(f32[4,25,1,24]{1,3,2,0:T(8,128)S(1)} %pad_maximum_fusion.35), channel_id=1, source_target_pairs={{0,2},{2,4},{4,6},{1,3},{3,5},{5,7},{8,10},{10,12},{12,14},{9,11},... | collective-permute-start | bytes 28808 | tf_op jit(solution)/shard_map/ppermute | solution.py:12
  49.9 1.7 collective-permute-done.7
  51.9 1.3 collective-permute-start.8
  54.2 1.8 maximum_maximum_fusion
  56.1 8.4 %slice.213 = f32[4,12,25,25]{1,3,2,0:T(8,128)} slice(f32[4,25,25,25]{1,3,2,0:T(8,128)S(1)} %maximum_maximum_fusion), slice={[0:4:1], [0:24:2], [0:25:1], [0:25:1]} | slice | bytes 240000 | tf_op jit(solution)/shard_map/slice | solution.py:48
  64.5 8.5 %slice.214 = f32[4,12,25,25]{1,3,2,0:T(8,128)} slice(f32[4,25,25,25]{1,3,2,0:T(8,128)S(1)} %maximum_maximum_fusion), slice={[0:4:1], [1:25:2], [0:25:1], [0:25:1]} | slice | bytes 240000 | tf_op jit(solution)/shard_map/slice | solution.py:49
  73.0 8.5 %slice.215 = f32[4,12,25,25]{1,3,2,0:T(8,128)} slice(f32[4,25,25,25]{1,3,2,0:T(8,128)S(1)} %maximum_maximum_fusion), slice={[0:4:1], [2:25:2], [0:25:1], [0:25:1]} | slice | bytes 240000 | tf_op jit(solution)/shard_map/slice | solution.py:50
  81.5 3.0 %multiply_add_fusion = f32[4,12,25,25]{1,3,2,0:T(8,128)S(1)} fusion(f32[4,12,25,25]{1,3,2,0:T(8,128)} %slice.215, f32[4,12,25,25]{1,3,2,0:T(8,128)} %slice.214, f32[4,12,25,25]{1,3,2,0:T(8,128)} %slice.213), kind=kLoop, calls=%fused_computation.3 | loop fusion | flops 150000 | bytes 480000 | tf_op jit(solution)/shard_map/add | solution.py:51
  85.7 4.3 %collective-permute-start.9 = (f32[4,1,12,12]{1,3,2,0:T(8,128)S(1)}, f32[4,1,12,12]{1,3,2,0:T(8,128)S(1)}, u32[]{:S(2)}, u32[]{:S(2)}) collective-permute-start(f32[4,1,12,12]{1,3,2,0:T(8,128)S(1)} %slice.265), channel_id=1, source_target_pairs={{0,8},{8,16},{16,24},{1,9},{9,17},{17,25},{2,10},{10,18},{18,26},{... | collective-permute-start | bytes 6920 | tf_op jit(solution)/shard_map/ppermute | solution.py:12
  89.9 1.8 all-gather
  91.8 7.0 %collective-permute-done.9 = f32[4,1,12,12]{1,3,2,0:T(8,128)S(1)} collective-permute-done((f32[4,1,12,12]{1,3,2,0:T(8,128)S(1)}, f32[4,1,12,12]{1,3,2,0:T(8,128)S(1)}, u32[]{:S(2)}, u32[]{:S(2)}) %collective-permute-start.9) | collective-permute-done | bytes 2336 | tf_op jit(solution)/shard_map/ppermute | solution.py:12
  98.9 5.1 %collective-permute-start.10 = (f32[4,13,1,12]{1,3,2,0:T(8,128)S(1)}, f32[4,13,1,12]{1,3,2,0:T(8,128)S(1)}, u32[]{:S(2)}, u32[]{:S(2)}) collective-permute-start(f32[4,13,1,12]{1,3,2,0:T(8,128)S(1)} %pad_maximum_fusion.39), channel_id=1, source_target_pairs={{0,2},{2,4},{4,6},{1,3},{3,5},{5,7},{8,10},{10,12},{12,14},{9,11},... | collective-permute-start | bytes 7496 | tf_op jit(solution)/shard_map/ppermute | solution.py:12
  104.1 1.5 collective-permute-done.10
  105.7 1.3 collective-permute-start.11
  108.5 0.9 slice.225
  109.4 1.0 slice.226
  110.4 1.0 slice.227
  113.9 1.3 collective-permute-start.12
  115.5 1.4 collective-permute-done.12
  117.0 1.8 all-gather.1
  119.3 1.3 collective-permute-start.13
  120.7 5.3 %collective-permute-done.13 = f32[4,30]{1,0:T(4,128)S(1)} collective-permute-done((f32[4,30]{1,0:T(4,128)S(1)}, f32[4,30]{1,0:T(4,128)S(1)}, u32[]{:S(2)}, u32[]{:S(2)}) %collective-permute-start.13) | collective-permute-done | bytes 512 | tf_op jit(solution)/shard_map/ppermute | solution.py:12
  126.2 13.6 %all-reduce = f32[4,240]{1,0:T(4,128)S(1)} all-reduce(f32[4,240]{1,0:T(4,128)S(1)} %fusion.36), channel_id=3, replica_groups=mesh['gx'=4,'gy'=4,'gz'=2] {'gy','gz'}, use_global_device_ids=true, to_apply=%region_0.1.clone | all-reduce | flops 960 | bytes 7680
  140.1 1.5 collective-permute-start.14
  141.6 4.5 %collective-permute-done.14 = f32[4,36]{1,0:T(4,128)S(1)} collective-permute-done((f32[4,36]{1,0:T(4,128)S(1)}, f32[4,36]{1,0:T(4,128)S(1)}, u32[]{:S(2)}, u32[]{:S(2)}) %collective-permute-start.14) | collective-permute-done | bytes 608 | tf_op jit(solution)/shard_map/ppermute | solution.py:12
  146.3 40.2 %all-reduce.1 = f32[4,1152]{1,0:T(4,128)S(1)} all-reduce(f32[4,1152]{1,0:T(4,128)S(1)} %fusion.68), channel_id=4, replica_groups=mesh['gx'=4,'gy'=4,'gz'=2] {'gx','gy','gz'}, use_global_device_ids=true, to_apply=%region_1.2.clone | all-reduce | flops 4608 | bytes 36864
  186.6 41.7 %all-gather.2 = f32[32,36,4]{1,2,0:T(4,128)S(1)} all-gather(f32[1,36,4]{1,2,0:T(4,128)S(1)} %dynamic-slice_bitcast_fusion), channel_id=1, replica_groups=mesh['gx'=4,'gy'=4,'gz'=2] {'gx','gy','gz'}, dimensions={0}, use_global_device_ids=true | all-gather | bytes 19008 | tf_op jit(solution)/shard_map/all_gather | solution.py:170
  228.7 1.3 collective-permute-start.15
  230.0 1.3 collective-permute-done.15
  231.5 7.4 %all-gather.3 = f32[8,30,4]{1,2,0:T(4,128)S(1)} all-gather(f32[1,30,4]{1,2,0:T(4,128)S(1)} %fusion.9), channel_id=1, replica_groups=mesh['gx'=4,'gy'=4,'gz'=2] {'gy','gz'}, dimensions={0}, use_global_device_ids=true | all-gather | bytes 4320 | tf_op jit(solution)/shard_map/all_gather | solution.py:175
  239.2 3.9 %collective-permute-start.16 = (f32[4,30]{1,0:T(4,128)S(1)}, f32[4,30]{1,0:T(4,128)S(1)}, u32[]{:S(2)}, u32[]{:S(2)}) collective-permute-start(f32[4,30]{1,0:T(4,128)S(1)} %fusion.34), channel_id=1, source_target_pairs={{0,2},{2,4},{4,6},{1,3},{3,5},{5,7},{8,10},{10,12},{12,14},{9,11},... | collective-permute-start | bytes 1448 | tf_op jit(solution)/shard_map/ppermute | solution.py:12
  243.1 1.3 collective-permute-done.16
  244.8 1.8 all-gather.4
  246.8 2.1 collective-permute-start.17
  250.6 1.1 scatter_custom_fusion
  251.9 1.3 collective-permute-start.18
  253.2 4.6 %collective-permute-done.18 = f32[4,1,6,6]{3,2,1,0:T(8,128)S(1)} collective-permute-done((f32[4,1,6,6]{3,2,1,0:T(8,128)S(1)}, f32[4,1,6,6]{3,2,1,0:T(8,128)S(1)}, u32[]{:S(2)}, u32[]{:S(2)}) %collective-permute-start.18) | collective-permute-done | bytes 608 | tf_op jit(solution)/shard_map/ppermute | solution.py:12
  257.8 1.3 collective-permute-start.19
  259.1 4.6 %collective-permute-done.19 = f32[4,7,1,6]{3,2,1,0:T(1,128)S(1)} collective-permute-done((f32[4,7,1,6]{3,2,1,0:T(1,128)S(1)}, f32[4,7,1,6]{3,2,1,0:T(1,128)S(1)}, u32[]{:S(2)}, u32[]{:S(2)}) %collective-permute-start.19) | collective-permute-done | bytes 704 | tf_op jit(solution)/shard_map/ppermute | solution.py:12
  263.7 1.3 collective-permute-start.20
  265.0 1.9 collective-permute-done.20
  268.3 1.3 collective-permute-start.21
  269.6 4.4 %collective-permute-done.21 = f32[4,1,12,12]{2,0,3,1:T(4,128)S(1)} collective-permute-done((f32[4,1,12,12]{2,0,3,1:T(4,128)S(1)}, f32[4,1,12,12]{2,0,3,1:T(4,128)S(1)}, u32[]{:S(2)}, u32[]{:S(2)}) %collective-permute-start.21) | collective-permute-done | bytes 2336 | tf_op jit(solution)/shard_map/ppermute | solution.py:12
  274.1 1.3 collective-permute-start.22
  275.4 10.5 %collective-permute-done.22 = f32[4,13,1,12]{2,0,3,1:T(4,128)S(1)} collective-permute-done((f32[4,13,1,12]{2,0,3,1:T(4,128)S(1)}, f32[4,13,1,12]{2,0,3,1:T(4,128)S(1)}, u32[]{:S(2)}, u32[]{:S(2)}) %collective-permute-start.22) | collective-permute-done | bytes 2528 | tf_op jit(solution)/shard_map/ppermute | solution.py:12
  286.0 1.3 collective-permute-start.23
  287.3 1.8 collective-permute-done.23
  289.6 0.9 copy.174
  290.7 0.9 copy.177
  292.2 1.4 copy.181
  (146 shorter events, 17.9 us)
Async XLA Ops:
  0.0 146.1 %copy-start = (f32[36,1152]{1,0:T(8,128)S(1)}, f32[36,1152]{1,0:T(8,128)}, u32[]{:S(2)}) copy-start(f32[36,1152]{1,0:T(8,128)} %param.27) | copy-start | bytes 497668
  0.9 8.5 %collective-permute-start = (f32[4,1,24,24]{3,2,1,0:T(8,128)S(1)}, f32[4,1,24,24]{3,2,1,0:T(8,128)S(1)}, u32[]{:S(2)}, u32[]{:S(2)}) collective-permute-start(f32[4,1,24,24]{3,2,1,0:T(8,128)S(1)} %get-tuple-element.10), channel_id=1, source_target_pairs={{8,0},{16,8},{24,16},{9,1},{17,9},{25,17},{10,2},{18,10},{26,18},{... | collective-permute-start | bytes 27656 | tf_op jit(solution)/shard_map/ppermute | solution.py:25
  2.2 7.9 %collective-permute-start.1 = (f32[4,1,24,24]{3,2,1,0:T(8,128)S(1)}, f32[4,1,24,24]{3,2,1,0:T(8,128)S(1)}, u32[]{:S(2)}, u32[]{:S(2)}) collective-permute-start(f32[4,1,24,24]{3,2,1,0:T(8,128)S(1)} %get-tuple-element.9), channel_id=1, source_target_pairs={{0,8},{8,16},{16,24},{1,9},{9,17},{17,25},{2,10},{10,18},{18,26},{... | collective-permute-start | bytes 27656 | tf_op jit(solution)/shard_map/ppermute | solution.py:23
  10.1 11.0 %copy-start.1 = (f32[4,1,24,24]{1,3,2,0:T(8,128)}, f32[4,1,24,24]{1,3,2,0:T(8,128)S(1)}, u32[]{:S(2)}) copy-start(f32[4,1,24,24]{1,3,2,0:T(8,128)S(1)} %copy.141) | copy-start | bytes 27652
  11.7 8.8 %copy-start.2 = (f32[4,1,24,24]{1,3,2,0:T(8,128)S(1)}, f32[4,1,24,24]{1,3,2,0:T(8,128)}, u32[]{:S(2)}) copy-start(f32[4,1,24,24]{1,3,2,0:T(8,128)} %copy.142) | copy-start | bytes 27652
  12.8 6.0 %collective-permute-start.2 = (f32[4,26,1,24]{1,3,2,0:T(8,128)S(1)}, f32[4,26,1,24]{1,3,2,0:T(8,128)S(1)}, u32[]{:S(2)}, u32[]{:S(2)}) collective-permute-start(f32[4,26,1,24]{1,3,2,0:T(8,128)S(1)} %get-tuple-element.8), channel_id=1, source_target_pairs={{2,0},{4,2},{6,4},{3,1},{5,3},{7,5},{10,8},{12,10},{14,12},{11,9},... | collective-permute-start | bytes 29960 | tf_op jit(solution)/shard_map/ppermute | solution.py:25
  14.1 11.5 %copy-start.4 = (f32[24,24,24]{2,1,0:T(8,128)S(1)}, f32[24,24,24]{2,1,0:T(8,128)}, u32[]{:S(2)}) copy-start(f32[24,24,24]{2,1,0:T(8,128)} %param.16) | copy-start | bytes 165892
  14.1 6.4 %collective-permute-start.3 = (f32[4,26,1,24]{1,3,2,0:T(8,128)S(1)}, f32[4,26,1,24]{1,3,2,0:T(8,128)S(1)}, u32[]{:S(2)}, u32[]{:S(2)}) collective-permute-start(f32[4,26,1,24]{1,3,2,0:T(8,128)S(1)} %get-tuple-element.7), channel_id=1, source_target_pairs={{0,2},{2,4},{4,6},{1,3},{3,5},{5,7},{8,10},{10,12},{12,14},{9,11},... | collective-permute-start | bytes 29960 | tf_op jit(solution)/shard_map/ppermute | solution.py:23
  21.1 7.3 %collective-permute-start.4 = (f32[4,26,26,1]{2,1,3,0:T(8,128)S(1)}, f32[4,26,26,1]{2,1,3,0:T(8,128)S(1)}, u32[]{:S(2)}, u32[]{:S(2)}) collective-permute-start(f32[4,26,26,1]{2,1,3,0:T(8,128)S(1)} %copy.147), channel_id=1, source_target_pairs={{1,0},{3,2},{5,4},{7,6},{9,8},{11,10},{13,12},{15,14},{17,16},{19,... | collective-permute-start | bytes 32456 | tf_op jit(solution)/shard_map/ppermute | solution.py:25
  22.5 6.0 %collective-permute-start.5 = (f32[4,26,26,1]{2,1,3,0:T(8,128)S(1)}, f32[4,26,26,1]{2,1,3,0:T(8,128)S(1)}, u32[]{:S(2)}, u32[]{:S(2)}) collective-permute-start(f32[4,26,26,1]{2,1,3,0:T(8,128)S(1)} %copy.149), channel_id=1, source_target_pairs={{0,1},{2,3},{4,5},{6,7},{8,9},{10,11},{12,13},{14,15},{16,17},{18,... | collective-permute-start | bytes 32456 | tf_op jit(solution)/shard_map/ppermute | solution.py:23
  39.0 5.7 %collective-permute-start.6 = (f32[4,1,24,24]{3,2,1,0:T(8,128)S(1)}, f32[4,1,24,24]{3,2,1,0:T(8,128)S(1)}, u32[]{:S(2)}, u32[]{:S(2)}) collective-permute-start(f32[4,1,24,24]{3,2,1,0:T(8,128)S(1)} %copy.152), channel_id=1, source_target_pairs={{0,8},{8,16},{16,24},{1,9},{9,17},{17,25},{2,10},{10,18},{18,26},{... | collective-permute-start | bytes 27656 | tf_op jit(solution)/shard_map/ppermute | solution.py:12
  45.3 8.8 %copy-start.3 = (f32[4,1,24,24]{1,3,2,0:T(8,128)}, f32[4,1,24,24]{1,3,2,0:T(8,128)S(1)}, u32[]{:S(2)}) copy-start(f32[4,1,24,24]{1,3,2,0:T(8,128)S(1)} %copy.153) | copy-start | bytes 27652
  45.3 4.6 %copy-start.14 = (s32[1,1,1,216]{3,2,1,0:T(1,128)S(1)}, s32[1,1,1,216]{3,2,1,0:T(1,128)}, u32[]{:S(2)}) copy-start(s32[1,1,1,216]{3,2,1,0:T(1,128)} %param.17) | copy-start | bytes 2596
  45.4 6.2 %collective-permute-start.7 = (f32[4,25,1,24]{1,3,2,0:T(8,128)S(1)}, f32[4,25,1,24]{1,3,2,0:T(8,128)S(1)}, u32[]{:S(2)}, u32[]{:S(2)}) collective-permute-start(f32[4,25,1,24]{1,3,2,0:T(8,128)S(1)} %pad_maximum_fusion.35), channel_id=1, source_target_pairs={{0,2},{2,4},{4,6},{1,3},{3,5},{5,7},{8,10},{10,12},{12,14},{9,11},... | collective-permute-start | bytes 28808 | tf_op jit(solution)/shard_map/ppermute | solution.py:12
  51.9 2.2 collective-permute-start.8
  85.4 4.6 %copy-start.13 = (f32[1,1,25,50]{3,1,2,0:T(1,128)S(1)}, f32[1,1,25,50]{3,1,2,0:T(1,128)}, u32[]{:S(2)}) copy-start(f32[1,1,25,50]{3,1,2,0:T(1,128)} %param.22) | copy-start | bytes 15004
  85.5 21.6 %copy-start.15 = (u32[32]{0:T(128)S(1)}, u32[32]{0:T(128)}, u32[]{:S(2)}) copy-start(u32[32]{0:T(128)} %constant.32) | copy-start | bytes 388
  85.7 13.1 %collective-permute-start.9 = (f32[4,1,12,12]{1,3,2,0:T(8,128)S(1)}, f32[4,1,12,12]{1,3,2,0:T(8,128)S(1)}, u32[]{:S(2)}, u32[]{:S(2)}) collective-permute-start(f32[4,1,12,12]{1,3,2,0:T(8,128)S(1)} %slice.265), channel_id=1, source_target_pairs={{0,8},{8,16},{16,24},{1,9},{9,17},{17,25},{2,10},{10,18},{18,26},{... | collective-permute-start | bytes 6920 | tf_op jit(solution)/shard_map/ppermute | solution.py:12
  98.9 6.7 %collective-permute-start.10 = (f32[4,13,1,12]{1,3,2,0:T(8,128)S(1)}, f32[4,13,1,12]{1,3,2,0:T(8,128)S(1)}, u32[]{:S(2)}, u32[]{:S(2)}) collective-permute-start(f32[4,13,1,12]{1,3,2,0:T(8,128)S(1)} %pad_maximum_fusion.39), channel_id=1, source_target_pairs={{0,2},{2,4},{4,6},{1,3},{3,5},{5,7},{8,10},{10,12},{12,14},{9,11},... | collective-permute-start | bytes 7496 | tf_op jit(solution)/shard_map/ppermute | solution.py:12
  105.7 2.7 collective-permute-start.11
  111.5 2.0 copy-start.5
  111.5 2.1 copy-start.9
  111.5 3.7 %copy-start.6 = (f32[1,1,1,125,72]{3,4,2,1,0:T(8,128)S(1)}, f32[1,1,1,125,72]{3,4,2,1,0:T(8,128)}, u32[]{:S(2)}) copy-start(f32[1,1,1,125,72]{3,4,2,1,0:T(8,128)} %param.21) | copy-start | bytes 108004
  111.5 3.8 %copy-start.8 = (f32[1,1,1,125,60]{3,2,4,1,0:T(1,128)S(1)}, f32[1,1,1,125,60]{3,2,4,1,0:T(1,128)}, u32[]{:S(2)}) copy-start(f32[1,1,1,125,60]{3,2,4,1,0:T(1,128)} %param.20) | copy-start | bytes 90004
  111.5 7.5 %copy-start.10 = (f32[1,1,1,25,60]{4,2,3,1,0:T(1,128)S(1)}, f32[1,1,1,25,60]{4,2,3,1,0:T(1,128)}, u32[]{:S(2)}) copy-start(f32[1,1,1,25,60]{4,2,3,1,0:T(1,128)} %param.23) | copy-start | bytes 18004
  111.6 9.0 %copy-start.11 = (f32[1,1,1,25,72]{4,2,3,1,0:T(1,128)S(1)}, f32[1,1,1,25,72]{4,2,3,1,0:T(1,128)}, u32[]{:S(2)}) copy-start(f32[1,1,1,25,72]{4,2,3,1,0:T(1,128)} %param.24) | copy-start | bytes 21604
  111.6 14.4 %copy-start.7 = (f32[1,30,240]{2,0,1:T(1,128)S(1)}, f32[1,30,240]{2,0,1:T(1,128)}, u32[]{:S(2)}) copy-start(f32[1,30,240]{2,0,1:T(1,128)} %param.25) | copy-start | bytes 86404
  111.6 28.3 %copy-start.12 = (f32[1,1,1,30,72]{4,2,3,1,0:T(1,128)S(1)}, f32[1,1,1,30,72]{4,2,3,1,0:T(1,128)}, u32[]{:S(2)}) copy-start(f32[1,1,1,30,72]{4,2,3,1,0:T(1,128)} %param.26) | copy-start | bytes 25924
  113.9 3.1 %collective-permute-start.12 = (f32[4,25]{1,0:T(4,128)S(1)}, f32[4,25]{1,0:T(4,128)S(1)}, u32[]{:S(2)}, u32[]{:S(2)}) collective-permute-start(f32[4,25]{1,0:T(4,128)S(1)} %slice.237), channel_id=1, source_target_pairs={{1,0},{3,2},{5,4},{7,6},{9,8},{11,10},{13,12},{15,14},{17,16},{19,... | collective-permute-start | bytes 1208 | tf_op jit(solution)/shard_map/ppermute | solution.py:12
  119.3 6.7 %collective-permute-start.13 = (f32[4,30]{1,0:T(4,128)S(1)}, f32[4,30]{1,0:T(4,128)S(1)}, u32[]{:S(2)}, u32[]{:S(2)}) collective-permute-start(f32[4,30]{1,0:T(4,128)S(1)} %slice.240), channel_id=1, source_target_pairs={{2,0},{4,2},{6,4},{3,1},{5,3},{7,5},{10,8},{12,10},{14,12},{11,9},... | collective-permute-start | bytes 1448 | tf_op jit(solution)/shard_map/ppermute | solution.py:12
  140.1 5.9 %collective-permute-start.14 = (f32[4,36]{1,0:T(4,128)S(1)}, f32[4,36]{1,0:T(4,128)S(1)}, u32[]{:S(2)}, u32[]{:S(2)}) collective-permute-start(f32[4,36]{1,0:T(4,128)S(1)} %slice.243), channel_id=1, source_target_pairs={{8,0},{16,8},{24,16},{9,1},{17,9},{25,17},{10,2},{18,10},{26,18},{... | collective-permute-start | bytes 1736 | tf_op jit(solution)/shard_map/ppermute | solution.py:12
  228.7 2.6 collective-permute-start.15
  239.2 5.2 %collective-permute-start.16 = (f32[4,30]{1,0:T(4,128)S(1)}, f32[4,30]{1,0:T(4,128)S(1)}, u32[]{:S(2)}, u32[]{:S(2)}) collective-permute-start(f32[4,30]{1,0:T(4,128)S(1)} %fusion.34), channel_id=1, source_target_pairs={{0,2},{2,4},{4,6},{1,3},{3,5},{5,7},{8,10},{10,12},{12,14},{9,11},... | collective-permute-start | bytes 1448 | tf_op jit(solution)/shard_map/ppermute | solution.py:12
  246.8 2.9 collective-permute-start.17
  251.9 5.9 %collective-permute-start.18 = (f32[4,1,6,6]{3,2,1,0:T(8,128)S(1)}, f32[4,1,6,6]{3,2,1,0:T(8,128)S(1)}, u32[]{:S(2)}, u32[]{:S(2)}) collective-permute-start(f32[4,1,6,6]{3,2,1,0:T(8,128)S(1)} %slice.270), channel_id=1, source_target_pairs={{8,0},{16,8},{24,16},{9,1},{17,9},{25,17},{10,2},{18,10},{26,18},{... | collective-permute-start | bytes 1736 | tf_op jit(solution)/shard_map/ppermute | solution.py:12
  257.8 5.9 %collective-permute-start.19 = (f32[4,7,1,6]{3,2,1,0:T(1,128)S(1)}, f32[4,7,1,6]{3,2,1,0:T(1,128)S(1)}, u32[]{:S(2)}, u32[]{:S(2)}) collective-permute-start(f32[4,7,1,6]{3,2,1,0:T(1,128)S(1)} %slice.271), channel_id=1, source_target_pairs={{2,0},{4,2},{6,4},{3,1},{5,3},{7,5},{10,8},{12,10},{14,12},{11,9},... | collective-permute-start | bytes 2024 | tf_op jit(solution)/shard_map/ppermute | solution.py:12
  263.7 3.2 %collective-permute-start.20 = (f32[4,7,7,1]{3,2,1,0:T(8,128)S(1)}, f32[4,7,7,1]{3,2,1,0:T(8,128)S(1)}, u32[]{:S(2)}, u32[]{:S(2)}) collective-permute-start(f32[4,7,7,1]{3,2,1,0:T(8,128)S(1)} %pad_maximum_fusion.26), channel_id=1, source_target_pairs={{1,0},{3,2},{5,4},{7,6},{9,8},{11,10},{13,12},{15,14},{17,16},{19,... | collective-permute-start | bytes 2360 | tf_op jit(solution)/shard_map/ppermute | solution.py:12
  268.3 5.7 %collective-permute-start.21 = (f32[4,1,12,12]{2,0,3,1:T(4,128)S(1)}, f32[4,1,12,12]{2,0,3,1:T(4,128)S(1)}, u32[]{:S(2)}, u32[]{:S(2)}) collective-permute-start(f32[4,1,12,12]{2,0,3,1:T(4,128)S(1)} %slice.278), channel_id=1, source_target_pairs={{8,0},{16,8},{24,16},{9,1},{17,9},{25,17},{10,2},{18,10},{26,18},{... | collective-permute-start | bytes 6920 | tf_op jit(solution)/shard_map/ppermute | solution.py:12
  274.1 11.8 %collective-permute-start.22 = (f32[4,13,1,12]{2,0,3,1:T(4,128)S(1)}, f32[4,13,1,12]{2,0,3,1:T(4,128)S(1)}, u32[]{:S(2)}, u32[]{:S(2)}) collective-permute-start(f32[4,13,1,12]{2,0,3,1:T(4,128)S(1)} %pad_maximum_fusion.22), channel_id=1, source_target_pairs={{2,0},{4,2},{6,4},{3,1},{5,3},{7,5},{10,8},{12,10},{14,12},{11,9},... | collective-permute-start | bytes 7496 | tf_op jit(solution)/shard_map/ppermute | solution.py:12
  286.0 3.1 %collective-permute-start.23 = (f32[4,13,13,1]{2,0,3,1:T(4,128)S(1)}, f32[4,13,13,1]{2,0,3,1:T(4,128)S(1)}, u32[]{:S(2)}, u32[]{:S(2)}) collective-permute-start(f32[4,13,13,1]{2,0,3,1:T(4,128)S(1)} %pad_maximum_fusion.40), channel_id=1, source_target_pairs={{1,0},{3,2},{5,4},{7,6},{9,8},{11,10},{13,12},{15,14},{17,16},{19,... | collective-permute-start | bytes 8120 | tf_op jit(solution)/shard_map/ppermute | solution.py:12
where the time goes:
time: 295 us; the launch traced here: 294 us
  blocking collectives  108 us (37%)
  starting transfers between devices  56.7 us (19%)
  waiting for transfers between devices  56.6 us (19%)
  local copies, waits for them, and re-layouts  48.2 us (16%)
  other arithmetic  18.5 us (6%)
  matrix products  3.58 us (1%)
    ppermute x18, waiting for transfers between devices, shifted(): return lax.ppermute(shard, axis, pairs)  54.9 us
    unnamed x2, blocking collectives  53.8 us
    all_gather x1, blocking collectives, per_device(): top_whole = lax.all_gather(top_own, ('gx', 'gy', 'gz'), axis=1, tiled=True)  41.7 us
    ppermute x18, starting transfers between devices, shifted(): return lax.ppermute(shard, axis, pairs)  39.5 us
    ppermute x3, starting transfers between devices, with_halo(): lax.ppermute(tail, axis, [(i, (i + 1) % count) for i in range(ends)])  13.3 us
    slice x4, local copies, waits for them, and re-layouts, weigh(): following = lax.slice_in_dim(extended, 2, length + 1, 2, dimension)  9.86 us
    slice x4, local copies, waits for them, and re-layouts, weigh(): centre = lax.slice_in_dim(extended, 1, length + 1, 2, dimension)  9.85 us
    slice x4, local copies, waits for them, and re-layouts, weigh(): previous = lax.slice_in_dim(extended, 0, length, 2, dimension)  9.6 us
  transfers between devices with their start and end apart: 24, of which 18 were waited for; matrix products, arithmetic and copies ran while one was open for 2% of the time, Pallas kernels for 0%

commit v1 on v0

v1 whole, which is shorter than its diff:
```python
import functools

import jax
import jax.numpy as jnp
import numpy as np
from jax import lax
from jax.experimental import pallas as pl
from jax.experimental.pallas import tpu as pltpu
from jax.sharding import PartitionSpec as P

AXES = ("gx", "gy", "gz")
LANES = 128
SIDES = (0, 1, -1)
MESH = pl.DeviceIdType.MESH
f32 = jnp.float32

SHARES = [
    (i, j, k)
    for i in SIDES
    for j in SIDES
    for k in SIDES
    if (i, j, k) != (0, 0, 0) and (i, j, k).count(-1) <= 1
]
RIMS = [(i, j, k) for i in (0, 1) for j in (0, 1) for k in (0, 1) if (i, j, k) != (0, 0, 0)]


def weight(k):
    return max(0, 4 - abs(k)) / 16.0


def weight_beside(k):
    return weight(k - 1) + weight(k + 1)


def dot(a, b):
    return jnp.dot(a, b, precision=lax.Precision.HIGHEST, preferred_element_type=f32)


def dot_back(a, b):
    return lax.dot_general(
        a, b, (((1,), (1,)), ((), ())),
        precision=lax.Precision.HIGHEST, preferred_element_type=f32,
    )


def coarse_at(side, row, count):
    if side == 0:
        return row if row < count else None
    if side == 1:
        return count if row == 0 else None
    return -1 if row == count - 1 else None


def restriction(fine, pad, stencil):
    count = fine // 4
    out = np.zeros((3, pad, fine), np.float32)
    for s, side in enumerate(SIDES):
        for row in range(pad):
            at = coarse_at(side, row, count)
            if at is not None:
                for y in range(fine):
                    out[s, row, y] = stencil(y - 4 * at)
    return out


def at_first(table):
    table = table.copy()
    table[0, 0, 0] -= weight(-1)
    return table


def interpolation(fine, pad):
    count = fine // 4
    out = np.zeros((2, fine, pad), np.float32)
    for y in range(fine):
        for at in (y // 4, y // 4 + 1):
            value = 1.0 - abs(y - 4 * at) / 4.0
            if at < count:
                out[0, y, at] = value
            else:
                out[1, y, 0] = value
    return out


def constants(rhs, ny, nz, slabs, pad_y, pad_z, rims):
    plain = restriction(ny, pad_y, weight)
    beside = restriction(ny, pad_y, weight_beside)
    eye = np.eye(slabs, dtype=np.float32)
    rows = np.stack([
        np.concatenate(
            [np.concatenate([np.kron(eye, plain[s]), np.kron(eye, b[s])], 1) for s in range(3)], 0
        )
        for b in (at_first(beside), beside)
    ])

    def over_lanes(table):
        out = np.zeros((3, rhs * nz, LANES), np.float32)
        for s in range(3):
            for r in range(rhs):
                out[s, r * nz:(r + 1) * nz, r * pad_z:(r + 1) * pad_z] = table[s].T
        return np.concatenate(list(out), 1)

    lanes = over_lanes(restriction(nz, pad_z, weight))
    table = restriction(nz, pad_z, weight_beside)
    lanes_beside = np.stack([over_lanes(at_first(table)), over_lanes(table)])
    grow = interpolation(nz, pad_z)
    wide = np.zeros((2, LANES, rhs * nz), np.float32)
    for s in range(2):
        for r in range(rhs):
            wide[s, r * pad_z:(r + 1) * pad_z, r * nz:(r + 1) * nz] = grow[s].T
    eye = np.eye(rims, dtype=np.float32)
    tall_of = interpolation(ny, pad_y)
    tall = np.stack([np.kron(eye, tall_of[s]) for s in range(2)])
    return rows, lanes, lanes_beside, wide, tall


def kernel(
    sizes,
    right_ref, u_ref, coef_ref, order_ref, leaf_ref, leaf_links, links_fs, links_ft, links_st,
    rows_first, rows_second, rows_top,
    mat_rows, mat_lanes, mat_beside, mat_wide, mat_tall,
    out_ref,
    packed, shares, total, share_in, prev, scatter_out, scatter_in, gather_in, whole, pairs,
    picked, ordered, rim, stage,
    share_send, share_recv, prev_send, prev_recv, s_send, s_recv, g_send, g_recv, r_send, r_recv,
):
    rhs, nx, ny, nz = u_ref.shape
    side = nx // 4
    side_y, side_z = ny // 4, nz // 4
    slabs = side + 2
    pad_y, pad_z = sizes["pad_y"], sizes["pad_z"]
    me = {a: lax.axis_index(a) for a in AXES}
    peers = sizes["peers"]
    rows_refs = (rows_first, rows_second, rows_top)
    groups = (("gz",), ("gy", "gz"), AXES)
    shift_axis = ("gz", "gy", "gx")
    counts = [int(np.prod([peers[a] for a in g])) for g in groups]

    def place(group):
        at = 0
        for a in group:
            at = at * peers[a] + me[a]
        return at

    def coords(group, at):
        found = {}
        for a in reversed(group):
            found[a] = at % peers[a]
            at = at // peers[a]
        return {a: found[a] if a in found else me[a] for a in AXES}

    prev_copies = []
    for level in range(3):
        axis = shift_axis[level]
        target = dict(me)
        target[axis] = (me[axis] + 1) % peers[axis]
        copy = pltpu.make_async_remote_copy(
            src_ref=rows_refs[level], dst_ref=prev[level],
            send_sem=prev_send.at[level], recv_sem=prev_recv.at[level],
            device_id=target, device_id_type=MESH,
        )
        prev_copies.append(copy)

        @pl.when(me[axis] < peers[axis] - 1)
        def _():
            copy.start()

        @pl.when(me[axis] == 0)
        def _():
            prev[level][...] = jnp.zeros(prev[level].shape, f32)

    half = slabs * ny
    for r in range(rhs):
        acc_p = {}
        acc_u = {}

        def add(acc, at, factor, value):
            term = factor * value
            acc[at] = acc[at] + term if at in acc else term

        for x in range(nx):
            u = u_ref[r, x]
            q = right_ref[r, x] - (6.0 + coef_ref[x]) * u
            for at in range(-1, side + 1):
                k = x - 4 * at
                if weight(k):
                    add(acc_p, at, weight(k), q)
                    add(acc_u, at, weight(k), u)
                if at == 0 and x == 0:
                    below = jnp.where(me["gx"] > 0, weight(-1), 0.0)
                    add(acc_p, at, weight(1) + below, u)
                elif weight_beside(k):
                    add(acc_p, at, weight_beside(k), u)
        for at in range(-1, side + 1):
            rows = slice((at + 1) * ny, (at + 2) * ny)
            packed[rows, r * nz:(r + 1) * nz] = acc_p[at]
            rows = slice(half + (at + 1) * ny, half + (at + 2) * ny)
            packed[rows, r * nz:(r + 1) * nz] = acc_u.get(at, jnp.zeros((ny, nz), f32))
    both = packed[...]
    at_y, at_z = jnp.minimum(me["gy"], 1), jnp.minimum(me["gz"], 1)
    a = dot(mat_rows[at_y], both)
    b = dot(mat_rows[1, :, :half], both[half:])
    c = dot(a, mat_lanes[...]) + dot(b, mat_beside[at_z])
    for s in range(3):
        for t in range(3):
            part = c[s * slabs * pad_y:(s + 1) * slabs * pad_y, t * LANES:(t + 1) * LANES]
            shares[s, t] = part.reshape(slabs, pad_y, LANES)

    def valid(step, sign):
        ok = None
        for a, d in zip(AXES, step):
            if d:
                at = me[a] + sign * d
                this = (at >= 0) & (at < peers[a])
                ok = this if ok is None else ok & this
        return ok

    def toward(step, sign):
        return {a: (me[a] + sign * d + peers[a]) % peers[a] for a, d in zip(AXES, step)}

    share_copies = []
    for n, step in enumerate(SHARES):
        dx, dy, dz = step
        cut = {0: pl.ds(1, side), 1: pl.ds(side + 1, 1), -1: pl.ds(0, 1)}[dx]
        copy = pltpu.make_async_remote_copy(
            src_ref=shares.at[SIDES.index(dy), SIDES.index(dz), cut],
            dst_ref=share_in[n],
            send_sem=share_send.at[n], recv_sem=share_recv.at[n],
            device_id=toward(step, 1), device_id_type=MESH,
        )
        share_copies.append(copy)

        @pl.when(valid(step, 1))
        def _():
            copy.start()

    total[...] = shares[0, 0, 1:side + 1]

    order = order_ref[...].astype(f32)
    first = jnp.floor((order + 0.5) / (side_y * side_z))
    rest = order - first * (side_y * side_z)
    second = jnp.floor((rest + 0.5) / side_z)
    third = rest - second * side_z
    cells = order.shape[1]
    spots = side * pad_y
    row_id = lax.broadcasted_iota(jnp.int32, (spots, cells), 0).astype(f32)
    row_hot = (row_id == first * pad_y + second).astype(f32)
    lane_id = lax.broadcasted_iota(jnp.int32, (LANES, cells), 0).astype(f32)

    def lane_hot(r):
        return (lane_id == third + r * pad_z).astype(f32)

    for n, step in enumerate(SHARES):
        @pl.when(valid(step, -1))
        def _():
            share_copies[n].wait_recv()
            if step[0] == 0:
                total[...] += share_in[n][...]
            elif step[0] == 1:
                total[0] += share_in[n][0]
            else:
                total[side - 1] += share_in[n][0]

    coarse = total[...].reshape(spots, LANES)
    for r in range(rhs):
        spread = dot(coarse, lane_hot(r))
        picked[r:r + 1, :] = jnp.sum(spread * row_hot, axis=0, keepdims=True)

    leaf = leaf_ref.shape[0]
    spans = [rows.shape[0] for rows in rows_refs]
    starts = [leaf, leaf + spans[0], leaf + spans[0] + spans[1]]
    leaf_solved = dot(picked[:, :leaf], leaf_ref[...])

    def all_slots(buffer, sem, count):
        return pltpu.make_async_copy(
            buffer.at[pl.ds(0, count - 1)], buffer.at[pl.ds(0, count - 1)], sem
        )

    def forward(level, toward_low):
        span, count, group = spans[level], counts[level], groups[level]
        axis = shift_axis[level]
        target = picked[:, starts[level]:starts[level] + span] - toward_low[:, :span]

        @pl.when(me[axis] > 0)
        def _():
            prev_copies[level].wait_recv()

        terms = dot(target, rows_refs[level][...]) - dot(toward_low[:, span:], prev[level][...])
        out, into = scatter_out[level], scatter_in[level]
        for d in range(count):
            out[d, :, :span] = terms[:, d * span:(d + 1) * span]
        mine = place(group)

        def send(k, carry):
            d = (mine + k) % count
            pltpu.make_async_remote_copy(
                src_ref=out.at[d], dst_ref=into.at[mine],
                send_sem=s_send.at[level], recv_sem=s_recv.at[level],
                device_id=coords(group, d), device_id_type=MESH,
            ).start()
            return carry

        lax.fori_loop(1, count, send, 0)
        into[mine] = out[mine]
        all_slots(into, s_recv.at[level], count).wait()
        return jnp.sum(into[...], axis=0)[:, :span]

    def backward(level, gap):
        span, count, group = spans[level], counts[level], groups[level]
        into = gather_in[level]
        own = stage[level]
        mine = place(group)
        own[:, :span] = gap

        def send(k, carry):
            d = (mine + k) % count
            pltpu.make_async_remote_copy(
                src_ref=own, dst_ref=into.at[mine],
                send_sem=g_send.at[level], recv_sem=g_recv.at[level],
                device_id=coords(group, d), device_id_type=MESH,
            ).start()
            return carry

        lax.fori_loop(1, count, send, 0)
        into[mine] = own[...]
        all_slots(into, g_recv.at[level], count).wait()
        full = whole[level]
        for d in range(count):
            full[:, d * span:(d + 1) * span] = into[d, :, :span]
        value = full[...]
        pair = pairs[level]
        back = dot_back(value, rows_refs[level][...])
        pair[:, :span] = back
        pair[:, span:] = dot_back(value, prev[level][...])
        return back, pair[...]

    to_first, to_second, to_top = (link[...] for link in leaf_links)
    first_own = forward(0, dot(leaf_solved, to_first))
    second_own = forward(1, dot(leaf_solved, to_second) + dot(first_own, links_fs[...]))
    top_own = forward(
        2,
        dot(leaf_solved, to_top) + dot(first_own, links_ft[...]) + dot(second_own, links_st[...]),
    )
    top_back, top_pair = backward(2, top_own)
    second_back, second_pair = backward(1, second_own - dot_back(top_pair, links_st[...]))
    first_back, first_pair = backward(
        0,
        first_own - dot_back(second_pair, links_fs[...]) - dot_back(top_pair, links_ft[...]),
    )
    leaf_gap = leaf_solved - dot_back(first_pair, to_first) - dot_back(second_pair, to_second)
    leaf_back = dot_back(leaf_gap - dot_back(top_pair, to_top), leaf_ref[...])
    ordered[:, :leaf] = leaf_back
    ordered[:, starts[0]:starts[1]] = first_back
    ordered[:, starts[1]:starts[2]] = second_back
    ordered[:, starts[2]:] = top_back

    cells_back = None
    for r in range(rhs):
        term = dot_back(row_hot * ordered[r:r + 1, :], lane_hot(r))
        cells_back = term if cells_back is None else cells_back + term
    rim[0, 0, 0:side] = cells_back.reshape(side, pad_y, LANES)

    rim_copies = []
    for n, step in enumerate(RIMS):
        dx, dy, dz = step
        source = rim.at[0, 0, pl.ds(0, 1 if dx else side)]
        landing = rim.at[dy, dz, pl.ds(side, 1) if dx else pl.ds(0, side)]
        copy = pltpu.make_async_remote_copy(
            src_ref=source, dst_ref=landing,
            send_sem=r_send.at[n], recv_sem=r_recv.at[n],
            device_id=toward(step, -1), device_id_type=MESH,
        )
        rim_copies.append(copy)

        @pl.when(valid(step, -1))
        def _():
            copy.start()

    for n, step in enumerate(RIMS):
        dx, dy, dz = step
        here = valid(step, 1)

        @pl.when(here)
        def _():
            rim_copies[n].wait_recv()

        @pl.when(jnp.logical_not(here))
        def _():
            if dx:
                rim[dy, dz, side] = jnp.zeros((pad_y, LANES), f32)
            else:
                rim[dy, dz, 0:side] = jnp.zeros((side, pad_y, LANES), f32)

    tall_rows = (side + 1) * pad_y
    grown = None
    for s in range(2):
        wide = dot(rim[s, 0].reshape(tall_rows, LANES), mat_wide[0])
        wide = wide + dot(rim[s, 1].reshape(tall_rows, LANES), mat_wide[1])
        term = dot(mat_tall[s], wide)
        grown = term if grown is None else grown + term
    for r in range(rhs):
        slices = [
            grown[at * ny:(at + 1) * ny, r * nz:(r + 1) * nz] for at in range(side + 1)
        ]
        for x in range(nx):
            at, k = x // 4, x % 4
            if k == 0:
                out_ref[r, x] = slices[at]
            else:
                out_ref[r, x] = (1 - k / 4) * slices[at] + (k / 4) * slices[at + 1]

    for level in range(3):
        axis = shift_axis[level]

        @pl.when(me[axis] < peers[axis] - 1)
        def _():
            prev_copies[level].wait_send()

        all_slots(scatter_out[level], s_send.at[level], counts[level]).wait()
        all_slots(gather_in[level], g_send.at[level], counts[level]).wait()
    for n, step in enumerate(SHARES):
        @pl.when(valid(step, 1))
        def _():
            share_copies[n].wait_send()
    for n, step in enumerate(RIMS):
        @pl.when(valid(step, -1))
        def _():
            rim_copies[n].wait_send()


def per_device(peers, right_side, iterate, coefficient, ordering, leaf_inverse, leaf_first,
               leaf_second, leaf_top, first_inverse, first_second, first_top, second_inverse,
               second_top, top_inverse):
    rhs, nx, ny, nz = iterate.shape
    side = nx // 4
    slabs = side + 2
    pad_y = -(-(ny // 4) // 8) * 8
    pad_z = LANES // rhs // 4 if nz // 4 <= LANES // rhs // 4 else LANES // rhs
    mats = constants(rhs, ny, nz, slabs, pad_y, pad_z, side + 1)
    flat = lambda m: m.reshape(m.shape[-2:])
    rows = [flat(first_inverse), flat(second_inverse), top_inverse]
    spans = [m.shape[0] for m in rows]
    counts = [m.shape[1] // m.shape[0] for m in rows]
    cells = ordering.shape[-1]
    vmem = lambda *shape: pltpu.VMEM(shape, f32)
    dma = lambda n: pltpu.SemaphoreType.DMA((n,))
    tile = (pad_y, LANES)
    sizes = {"peers": peers, "pad_y": pad_y, "pad_z": pad_z}
    operands = (
        right_side, iterate, coefficient, ordering.reshape(1, cells), flat(leaf_inverse),
        (flat(leaf_first), flat(leaf_second), flat(leaf_top)),
        flat(first_second), flat(first_top), flat(second_top), *rows,
        *[jnp.asarray(m) for m in mats],
    )
    in_vmem = pl.BlockSpec(memory_space=pltpu.VMEM)
    return pl.pallas_call(
        functools.partial(kernel, sizes),
        out_shape=jax.ShapeDtypeStruct(iterate.shape, f32),
        in_specs=jax.tree.map(lambda _: in_vmem, operands),
        out_specs=in_vmem,
        scratch_shapes=[
            vmem(2 * slabs * ny, rhs * nz),
            vmem(3, 3, slabs, *tile),
            vmem(side, *tile),
            [vmem(side if step[0] == 0 else 1, *tile) for step in SHARES],
            [vmem(*m.shape) for m in rows],
            [vmem(n, rhs, LANES) for n in counts],
            [vmem(n, rhs, LANES) for n in counts],
            [vmem(n, rhs, LANES) for n in counts],
            [vmem(rhs, m.shape[1]) for m in rows],
            [vmem(rhs, 2 * s) for s in spans],
            vmem(rhs, cells),
            vmem(rhs, cells),
            vmem(2, 2, side + 1, *tile),
            [vmem(rhs, LANES) for _ in rows],
            dma(len(SHARES)), dma(len(SHARES)), dma(3), dma(3), dma(3), dma(3), dma(3), dma(3),
            dma(len(RIMS)), dma(len(RIMS)),
        ],
        compiler_params=pltpu.CompilerParams(has_side_effects=True),
    )(*operands)


def solution(mesh):
    peers = dict(mesh.shape)
    return jax.shard_map(
        functools.partial(per_device, peers),
        mesh=mesh,
        in_specs=(
            P(None, "gx", "gy", "gz"),
            P(None, "gx", "gy", "gz"),
            P("gx", "gy", "gz"),
            P("gx", "gy", "gz", None),
            P("gx", "gy", "gz", None, None),
            P("gx", "gy", "gz", None, None),
            P("gx", "gy", "gz", None, None),
            P("gx", "gy", "gz", None, None),
            P("gx", "gy", "gz", None),
            P("gx", "gy", "gz", None, None),
            P("gx", "gy", "gz", None, None),
            P("gx", ("gy", "gz"), None),
            P("gx", "gy", "gz", None, None),
            P(("gx", "gy", "gz"), None),
        ),
        out_specs=P(None, "gx", "gy", "gz"),
        check_vma=False,
    )
```

time: 295 us -> 62.9 us (0.21)
  blocking collectives: 108 us -> 0 us
  starting transfers between devices: 56.7 us -> 0 us
  waiting for transfers between devices: 56.6 us -> 0 us
  Pallas kernels: 0 us -> 47.4 us
  local copies, waits for them, and re-layouts: 48.2 us -> 14.8 us
  other arithmetic: 18.5 us -> 0 us
  matrix products: 3.58 us -> 0 us
    ppermute x24 -> x0, starting transfers between devices: 56.7 us -> none  [the longest x18 39.5 us: shifted(): return lax.ppermute(shard, axis, pairs)]
    ppermute x24 -> x0, waiting for transfers between devices: 56.6 us -> none  [the longest x18 54.9 us: shifted(): return lax.ppermute(shard, axis, pairs)]
    all_gather x5 -> x0, blocking collectives: 54.7 us -> none  [the longest x1 41.7 us: per_device(): top_whole = lax.all_gather(top_own, ('gx', 'gy', 'gz'), axis=1, tiled=True)]
    unnamed x2 -> x0, blocking collectives: 53.8 us -> none
    pallas_call x0 -> x1, Pallas kernels: none -> 47.4 us  [per_device(): pl.pallas_call(functools.partial(kernel, sizes), out_shape=jax.ShapeDtype...]
    slice x25 -> x0, local copies, waits for them, and re-layouts: 31.9 us -> none  [the longest x4 9.86 us: weigh(): following = lax.slice_in_dim(extended, 2, length + 1, 2, dimension)]
    sub x1 -> x0, other arithmetic: 9.37 us -> none  [residual_of(): return right_side - ((6.0 + coefficient) * iterate - beside)]
    unnamed x42 -> x10, local copies, waits for them, and re-layouts: 5.5 us -> 14.8 us
  transfers between devices with their start and end apart: 24 -> 0, of which waited for: 18 -> 0; matrix products, arithmetic and copies ran while one was open for 2% -> 0% of each run, Pallas kernels for 0% -> 0%
where the time goes in v1:
time: 62.9 us; the launch traced here: 62.2 us
  Pallas kernels  47.4 us (75%)
  local copies, waits for them, and re-layouts  14.8 us (24%)
    pallas_call x1, Pallas kernels, per_device(): pl.pallas_call(functools.partial(kernel, sizes), out_shape=jax.ShapeDtype...  47.4 us
    unnamed x10, local copies, waits for them, and re-layouts  14.8 us

profile of v1, /device:TPU:0, one launch (start us, length us, event | category | flops | bytes accessed | tf_op | source)
XLA Modules:
  0.0 62.2 jit_solution(2871438292418684178)
XLA Ops:
  0.0 1.3 %copy.37 = f32[1,1,25,50]{3,2,1,0:T(8,128)} copy(f32[1,1,25,50]{3,1,2,0:T(1,128)} %param.27) | data formatting | bytes 10000
  1.3 1.3 %copy.40 = f32[1,1,1,25,60]{4,3,2,1,0:T(8,128)} copy(f32[1,1,1,25,60]{4,2,3,1,0:T(1,128)} %param.28) | data formatting | bytes 12000
  2.6 1.3 %copy.39 = f32[1,1,1,25,72]{4,3,2,1,0:T(8,128)} copy(f32[1,1,1,25,72]{4,2,3,1,0:T(1,128)} %param.29) | data formatting | bytes 14400
  3.9 1.3 %copy.38 = f32[1,1,1,30,72]{4,3,2,1,0:T(8,128)} copy(f32[1,1,1,30,72]{4,2,3,1,0:T(1,128)} %param.31) | data formatting | bytes 17280
  5.2 1.4 %copy.36 = f32[1,30,240]{2,1,0:T(8,128)} copy(f32[1,30,240]{2,0,1:T(1,128)} %param.30) | data formatting | bytes 57600
  6.6 1.5 %copy.35 = f32[1,1,1,125,125]{4,3,2,1,0:T(8,128)} copy(f32[1,1,1,125,125]{4,2,3,1,0:T(1,128)} %param.23) | data formatting | bytes 125000
  8.1 1.5 %copy.20 = f32[1,1,1,125,50]{4,3,2,1,0:T(8,128)} copy(f32[1,1,1,125,50]{3,2,4,1,0:T(1,128)} %param.24) | data formatting | bytes 50000 | tf_op args[5]
  9.5 1.5 %copy.21 = f32[1,1,1,125,60]{4,3,2,1,0:T(8,128)} copy(f32[1,1,1,125,60]{3,2,4,1,0:T(1,128)} %param.25) | data formatting | bytes 60000 | tf_op args[6]
  11.0 1.5 %copy.22 = f32[1,1,1,125,72]{4,3,2,1,0:T(8,128)} copy(f32[1,1,1,125,72]{3,4,2,1,0:T(8,128)} %param.26) | data formatting | bytes 72000 | tf_op args[7]
  12.5 47.4 %shard_map.181 = f32[4,24,24,24]{3,2,1,0:T(8,128)} custom-call(f32[4,24,24,24]{3,2,1,0:T(8,128)} %right_ref.1, f32[4,24,24,24]{3,2,1,0:T(8,128)} %u_ref.1, f32[24,24,24]{2,1,0:T(8,128)} %coef_ref.1, s32[1,216]{1,0:T(1,128)} %bitcast.31, f32[125,125]{1,0:T(8,128)} %bitcast.22, f32[125,50]{1,0:T(8,128)} %bitcast.23, f32[125,60]{1,0:T(8,128)} %bitcast.24, ...), custom_call_target="tpu_custom_call" | custom-call | tf_op jit(solution)/shard_map/pallas_call | solution.py:456
  59.9 2.4 %copy.42 = f32[4,24,24,24]{3,2,1,0:T(8,128)} copy(f32[4,24,24,24]{3,2,1,0:T(8,128)} %shard_map.181) | data formatting | bytes 442368

commit v2 on v1

--- a/solution.py
+++ b/solution.py
@@ -13,6 +13,7 @@
 SIDES = (0, 1, -1)
 MESH = pl.DeviceIdType.MESH
 f32 = jnp.float32
+bf16 = jnp.bfloat16
 
 SHARES = [
     (i, j, k)
@@ -32,15 +33,37 @@
     return weight(k - 1) + weight(k + 1)
 
 
-def dot(a, b):
-    return jnp.dot(a, b, precision=lax.Precision.HIGHEST, preferred_element_type=f32)
+def single(a, b):
+    return jnp.dot(a, b, preferred_element_type=f32)
+
+
+def single_back(a, b):
+    return lax.dot_general(a, b, (((1,), (1,)), ((), ())), preferred_element_type=f32)
+
+
+def halves(x):
+    high = x.astype(bf16)
+    return high, (x - high.astype(f32)).astype(bf16)
+
+
+def stacked(x):
+    high = x.astype(bf16).astype(f32)
+    return jnp.concatenate([high, x - high], axis=0).astype(bf16)
+
+
+def dot_exact(a, b, product=single):
+    high, low = halves(a)
+    return product(high, b) + product(low, b)
+
+
+def dot(a, b, product=single):
+    count = a.shape[0]
+    both = product(stacked(a), b[0][...])
+    return both[:count] + both[count:] + product(a.astype(bf16), b[1][...])
 
 
 def dot_back(a, b):
-    return lax.dot_general(
-        a, b, (((1,), (1,)), ((), ())),
-        precision=lax.Precision.HIGHEST, preferred_element_type=f32,
-    )
+    return dot(a, b, single_back)
 
 
 def coarse_at(side, row, count):
@@ -116,10 +139,11 @@
 
 def kernel(
     sizes,
-    right_ref, u_ref, coef_ref, order_ref, leaf_ref, leaf_links, links_fs, links_ft, links_st,
-    rows_first, rows_second, rows_top,
+    right_ref, u_ref, coef_ref, order_ref, leaf_raw, leaf_first_raw, leaf_second_raw,
+    leaf_top_ref, fs_raw, ft_raw, st_raw, rows_first, rows_second, rows_top,
     mat_rows, mat_lanes, mat_beside, mat_wide, mat_tall,
     out_ref,
+    split_leaf, split_links, split_fs, split_ft, split_st, split_rows, left,
     packed, shares, total, share_in, prev, scatter_out, scatter_in, gather_in, whole, pairs,
     picked, ordered, rim, stage,
     share_send, share_recv, prev_send, prev_recv, s_send, s_recv, g_send, g_recv, r_send, r_recv,
@@ -163,7 +187,8 @@
 
         @pl.when(me[axis] < peers[axis] - 1)
         def _():
-            copy.start()
+            if level < 2:
+                copy.start()
 
         @pl.when(me[axis] == 0)
         def _():
@@ -198,9 +223,10 @@
             packed[rows, r * nz:(r + 1) * nz] = acc_u.get(at, jnp.zeros((ny, nz), f32))
     both = packed[...]
     at_y, at_z = jnp.minimum(me["gy"], 1), jnp.minimum(me["gz"], 1)
-    a = dot(mat_rows[at_y], both)
-    b = dot(mat_rows[1, :, :half], both[half:])
-    c = dot(a, mat_lanes[...]) + dot(b, mat_beside[at_z])
+    high, low = halves(both)
+    a = single(mat_rows[at_y], high) + single(mat_rows[at_y], low)
+    b = single(mat_rows[1, :, :half], high[half:]) + single(mat_rows[1, :, :half], low[half:])
+    c = dot_exact(a, mat_lanes[...]) + dot_exact(b, mat_beside[at_z])
     for s in range(3):
         for t in range(3):
             part = c[s * slabs * pad_y:(s + 1) * slabs * pad_y, t * LANES:(t + 1) * LANES]
@@ -234,7 +260,49 @@
         def _():
             copy.start()
 
+    @pl.when(me[shift_axis[2]] < peers[shift_axis[2]] - 1)
+    def _():
+        prev_copies[2].start()
+
     total[...] = shares[0, 0, 1:side + 1]
+
+    def keep(where, value):
+        where[0][...], where[1][...] = halves(value)
+
+    def rows_of(raw):
+        return raw[:, 0, :] if len(raw.shape) == 3 else raw[...]
+
+    spans = [rows.shape[0] for rows in rows_refs]
+    seats = [split_rows[level][0].shape[0] // 2 for level in range(3)]
+
+    def keep_rows(level, at, value):
+        high, low = halves(value)
+        split_rows[level][0][at:at + spans[level], :] = high
+        split_rows[level][1][at:at + spans[level], :] = low
+
+    keep(split_leaf, rows_of(leaf_raw))
+    for where, raw in zip(split_links, (leaf_first_raw, leaf_second_raw, leaf_top_ref)):
+        keep(where, rows_of(raw))
+    keep(split_fs, rows_of(fs_raw))
+    keep(split_ft, rows_of(ft_raw))
+    keep(split_st, rows_of(st_raw))
+    for level in range(3):
+        for part in split_rows[level]:
+            part[...] = jnp.zeros(part.shape, bf16)
+        left[level][...] = jnp.zeros(left[level].shape, f32)
+        keep_rows(level, 0, rows_of(rows_refs[level]))
+
+    def settle(level):
+        axis = shift_axis[level]
+
+        @pl.when(me[axis] > 0)
+        def _():
+            prev_copies[level].wait_recv()
+
+        keep_rows(level, seats[level], rows_of(prev[level]))
+
+    settle(0)
+    settle(1)
 
     order = order_ref[...].astype(f32)
     first = jnp.floor((order + 0.5) / (side_y * side_z))
@@ -248,7 +316,7 @@
     lane_id = lax.broadcasted_iota(jnp.int32, (LANES, cells), 0).astype(f32)
 
     def lane_hot(r):
-        return (lane_id == third + r * pad_z).astype(f32)
+        return (lane_id == third + r * pad_z).astype(f32).astype(bf16)
 
     for n, step in enumerate(SHARES):
         @pl.when(valid(step, -1))
@@ -263,13 +331,12 @@
 
     coarse = total[...].reshape(spots, LANES)
     for r in range(rhs):
-        spread = dot(coarse, lane_hot(r))
+        spread = dot_exact(coarse, lane_hot(r))
         picked[r:r + 1, :] = jnp.sum(spread * row_hot, axis=0, keepdims=True)
 
-    leaf = leaf_ref.shape[0]
-    spans = [rows.shape[0] for rows in rows_refs]
+    leaf = leaf_raw.shape[0]
     starts = [leaf, leaf + spans[0], leaf + spans[0] + spans[1]]
-    leaf_solved = dot(picked[:, :leaf], leaf_ref[...])
+    leaf_solved = dot(picked[:, :leaf], split_leaf)
 
     def all_slots(buffer, sem, count):
         return pltpu.make_async_copy(
@@ -278,14 +345,11 @@
 
     def forward(level, toward_low):
         span, count, group = spans[level], counts[level], groups[level]
-        axis = shift_axis[level]
+        seat = seats[level]
         target = picked[:, starts[level]:starts[level] + span] - toward_low[:, :span]
-
-        @pl.when(me[axis] > 0)
-        def _():
-            prev_copies[level].wait_recv()
-
-        terms = dot(target, rows_refs[level][...]) - dot(toward_low[:, span:], prev[level][...])
+        left[level][:, :span] = target
+        left[level][:, seat:seat + span] = -toward_low[:, span:]
+        terms = dot(left[level][...], split_rows[level])
         out, into = scatter_out[level], scatter_in[level]
         for d in range(count):
             out[d, :, :span] = terms[:, d * span:(d + 1) * span]
@@ -302,8 +366,11 @@
 
         lax.fori_loop(1, count, send, 0)
         into[mine] = out[mine]
-        all_slots(into, s_recv.at[level], count).wait()
-        return jnp.sum(into[...], axis=0)[:, :span]
+
+    def forward_end(level):
+        into = scatter_in[level]
+        all_slots(into, s_recv.at[level], counts[level]).wait()
+        return jnp.sum(into[...], axis=0)[:, :spans[level]]
 
     def backward(level, gap):
         span, count, group = spans[level], counts[level], groups[level]
@@ -323,32 +390,43 @@
 
         lax.fori_loop(1, count, send, 0)
         into[mine] = own[...]
+
+    def backward_end(level):
+        span, count, seat = spans[level], counts[level], seats[level]
+        into = gather_in[level]
         all_slots(into, g_recv.at[level], count).wait()
         full = whole[level]
         for d in range(count):
             full[:, d * span:(d + 1) * span] = into[d, :, :span]
         value = full[...]
         pair = pairs[level]
-        back = dot_back(value, rows_refs[level][...])
+        solved = dot_back(value, split_rows[level])
+        back = solved[:, :span]
         pair[:, :span] = back
-        pair[:, span:] = dot_back(value, prev[level][...])
+        pair[:, span:] = solved[:, seat:seat + span]
         return back, pair[...]
 
-    to_first, to_second, to_top = (link[...] for link in leaf_links)
-    first_own = forward(0, dot(leaf_solved, to_first))
-    second_own = forward(1, dot(leaf_solved, to_second) + dot(first_own, links_fs[...]))
-    top_own = forward(
-        2,
-        dot(leaf_solved, to_top) + dot(first_own, links_ft[...]) + dot(second_own, links_st[...]),
-    )
-    top_back, top_pair = backward(2, top_own)
-    second_back, second_pair = backward(1, second_own - dot_back(top_pair, links_st[...]))
-    first_back, first_pair = backward(
-        0,
-        first_own - dot_back(second_pair, links_fs[...]) - dot_back(top_pair, links_ft[...]),
-    )
-    leaf_gap = leaf_solved - dot_back(first_pair, to_first) - dot_back(second_pair, to_second)
-    leaf_back = dot_back(leaf_gap - dot_back(top_pair, to_top), leaf_ref[...])
+    to_first, to_second, to_top = split_links
+    forward(0, dot_back(leaf_solved, to_first))
+    second_low = dot_back(leaf_solved, to_second)
+    top_low = dot_back(leaf_solved, to_top)
+    first_own = forward_end(0)
+    forward(1, second_low + dot(first_own, split_fs))
+    top_low = top_low + dot(first_own, split_ft)
+    settle(2)
+    second_own = forward_end(1)
+    forward(2, top_low + dot(second_own, split_st))
+    top_own = forward_end(2)
+    backward(2, top_own)
+    top_back, top_pair = backward_end(2)
+    backward(1, second_own - dot_back(top_pair, split_st))
+    first_gap = first_own - dot_back(top_pair, split_ft)
+    leaf_gap = leaf_solved - dot(top_pair, to_top)
+    second_back, second_pair = backward_end(1)
+    backward(0, first_gap - dot_back(second_pair, split_fs))
+    leaf_gap = leaf_gap - dot(second_pair, to_second)
+    first_back, first_pair = backward_end(0)
+    leaf_back = dot_back(leaf_gap - dot(first_pair, to_first), split_leaf)
     ordered[:, :leaf] = leaf_back
     ordered[:, starts[0]:starts[1]] = first_back
     ordered[:, starts[1]:starts[2]] = second_back
@@ -356,7 +434,7 @@
 
     cells_back = None
     for r in range(rhs):
-        term = dot_back(row_hot * ordered[r:r + 1, :], lane_hot(r))
+        term = dot_exact(row_hot * ordered[r:r + 1, :], lane_hot(r), single_back)
         cells_back = term if cells_back is None else cells_back + term
     rim[0, 0, 0:side] = cells_back.reshape(side, pad_y, LANES)
 
@@ -394,9 +472,10 @@
     tall_rows = (side + 1) * pad_y
     grown = None
     for s in range(2):
-        wide = dot(rim[s, 0].reshape(tall_rows, LANES), mat_wide[0])
-        wide = wide + dot(rim[s, 1].reshape(tall_rows, LANES), mat_wide[1])
-        term = dot(mat_tall[s], wide)
+        wide = dot_exact(rim[s, 0].reshape(tall_rows, LANES), mat_wide[0])
+        wide = wide + dot_exact(rim[s, 1].reshape(tall_rows, LANES), mat_wide[1])
+        high, low = halves(wide)
+        term = single(mat_tall[s], high) + single(mat_tall[s], low)
         grown = term if grown is None else grown + term
     for r in range(rhs):
         slices = [
@@ -437,20 +516,26 @@
     pad_y = -(-(ny // 4) // 8) * 8
     pad_z = LANES // rhs // 4 if nz // 4 <= LANES // rhs // 4 else LANES // rhs
     mats = constants(rhs, ny, nz, slabs, pad_y, pad_z, side + 1)
+    flip = lambda m: jnp.swapaxes(m, -1, -2)
     flat = lambda m: m.reshape(m.shape[-2:])
-    rows = [flat(first_inverse), flat(second_inverse), top_inverse]
+    single_rows = lambda m: m.reshape(m.shape[-2], 1, m.shape[-1])
+    rows = [single_rows(first_inverse), single_rows(second_inverse), top_inverse]
     spans = [m.shape[0] for m in rows]
-    counts = [m.shape[1] // m.shape[0] for m in rows]
+    widths = [m.shape[-1] for m in rows]
+    counts = [w // s for w, s in zip(widths, spans)]
+    seats = [-(-s // 16) * 16 for s in spans]
+    leaf = leaf_inverse.shape[-1]
     cells = ordering.shape[-1]
     vmem = lambda *shape: pltpu.VMEM(shape, f32)
+    split = lambda *shape: [pltpu.VMEM(shape, bf16)] * 2
     dma = lambda n: pltpu.SemaphoreType.DMA((n,))
     tile = (pad_y, LANES)
     sizes = {"peers": peers, "pad_y": pad_y, "pad_z": pad_z}
     operands = (
-        right_side, iterate, coefficient, ordering.reshape(1, cells), flat(leaf_inverse),
-        (flat(leaf_first), flat(leaf_second), flat(leaf_top)),
-        flat(first_second), flat(first_top), flat(second_top), *rows,
-        *[jnp.asarray(m) for m in mats],
+        right_side, iterate, coefficient, ordering.reshape(1, cells), single_rows(leaf_inverse),
+        single_rows(flip(leaf_first)), single_rows(flip(leaf_second)), flat(flip(leaf_top)),
+        single_rows(first_second), single_rows(first_top), single_rows(second_top), *rows,
+        *[jnp.asarray(m, bf16) for m in mats],
     )
     in_vmem = pl.BlockSpec(memory_space=pltpu.VMEM)
     return pl.pallas_call(
@@ -459,6 +544,13 @@
         in_specs=jax.tree.map(lambda _: in_vmem, operands),
         out_specs=in_vmem,
         scratch_shapes=[
+            split(leaf, leaf),
+            [split(2 * s, leaf) for s in spans],
+            split(spans[0], 2 * spans[1]),
+            split(spans[0], 2 * spans[2]),
+            split(spans[1], 2 * spans[2]),
+            [split(2 * seat, w) for seat, w in zip(seats, widths)],
+            [vmem(rhs, 2 * seat) for seat in seats],
             vmem(2 * slabs * ny, rhs * nz),
             vmem(3, 3, slabs, *tile),
             vmem(side, *tile),
@@ -467,7 +559,7 @@
             [vmem(n, rhs, LANES) for n in counts],
             [vmem(n, rhs, LANES) for n in counts],
             [vmem(n, rhs, LANES) for n in counts],
-            [vmem(rhs, m.shape[1]) for m in rows],
+            [vmem(rhs, w) for w in widths],
             [vmem(rhs, 2 * s) for s in spans],
             vmem(rhs, cells),
             vmem(rhs, cells),

time: 62.9 us -> 45.5 us (0.72)
  local copies, waits for them, and re-layouts: 14.8 us -> 2.36 us
  Pallas kernels: 47.4 us -> 43 us
    unnamed x10 -> x1, local copies, waits for them, and re-layouts: 14.8 us -> 2.36 us
    pallas_call x1, Pallas kernels: 47.4 us -> 43 us  [per_device(): pl.pallas_call(functools.partial(kernel, sizes), out_shape=jax.ShapeDtype...]
where the time goes in v2:
time: 45.5 us; the launch traced here: 45.4 us
  Pallas kernels  43 us (95%)
  local copies, waits for them, and re-layouts  2.36 us (5%)
    pallas_call x1, Pallas kernels, per_device(): pl.pallas_call(functools.partial(kernel, sizes), out_shape=jax.ShapeDtype...  43 us
    unnamed x1, local copies, waits for them, and re-layouts  2.36 us

profile of v2, /device:TPU:0, one launch (start us, length us, event | category | flops | bytes accessed | tf_op | source)
XLA Modules:
  0.0 45.4 jit_solution(10735029167966784377)
XLA Ops:
  0.0 43.0 %shard_map.181 = f32[4,24,24,24]{3,2,1,0:T(8,128)} custom-call(f32[4,24,24,24]{3,2,1,0:T(8,128)} %right_ref.1, f32[4,24,24,24]{3,2,1,0:T(8,128)} %u_ref.1, f32[24,24,24]{2,1,0:T(8,128)} %coef_ref.1, s32[1,216]{1,0:T(1,128)} %bitcast.29, f32[125,1,125]{2,1,0:T(1,128)} %bitcast.20, f32[50,1,125]{2,1,0:T(1,128)} %bitcast.24, f32[60,1,125]{2,1,0:T(1,128)} %bitcast.22, ...), custom_call_target="tpu_custom_call" | custom-call | tf_op jit(solution)/shard_map/pallas_call | solution.py:541
  43.0 2.4 %copy.23 = f32[4,24,24,24]{3,2,1,0:T(8,128)} copy(f32[4,24,24,24]{3,2,1,0:T(8,128)} %shard_map.181) | data formatting | bytes 442368

commit v3 on v2

--- a/solution.py
+++ b/solution.py
@@ -173,6 +173,17 @@
             at = at // peers[a]
         return {a: found[a] if a in found else me[a] for a in AXES}
 
+    barrier = pltpu.get_barrier_semaphore()
+    everyone, myself = counts[2], place(AXES)
+
+    def greet(k, carry):
+        pl.semaphore_signal(
+            barrier, inc=1, device_id=coords(AXES, (myself + k) % everyone), device_id_type=MESH
+        )
+        return carry
+
+    lax.fori_loop(1, everyone, greet, 0)
+
     prev_copies = []
     for level in range(3):
         axis = shift_axis[level]
@@ -184,11 +195,6 @@
             device_id=target, device_id_type=MESH,
         )
         prev_copies.append(copy)
-
-        @pl.when(me[axis] < peers[axis] - 1)
-        def _():
-            if level < 2:
-                copy.start()
 
         @pl.when(me[axis] == 0)
         def _():
@@ -244,6 +250,12 @@
     def toward(step, sign):
         return {a: (me[a] + sign * d + peers[a]) % peers[a] for a, d in zip(AXES, step)}
 
+    pl.semaphore_wait(barrier, everyone - 1)
+    for level in range(2):
+        @pl.when(me[shift_axis[level]] < peers[shift_axis[level]] - 1)
+        def _():
+            prev_copies[level].start()
+
     share_copies = []
     for n, step in enumerate(SHARES):
         dx, dy, dz = step
@@ -477,9 +489,33 @@
         high, low = halves(wide)
         term = single(mat_tall[s], high) + single(mat_tall[s], low)
         grown = term if grown is None else grown + term
+    out_ref[...] = grown
+
+    for level in range(3):
+        axis = shift_axis[level]
+
+        @pl.when(me[axis] < peers[axis] - 1)
+        def _():
+            prev_copies[level].wait_send()
+
+        all_slots(scatter_out[level], s_send.at[level], counts[level]).wait()
+        all_slots(gather_in[level], g_send.at[level], counts[level]).wait()
+    for n, step in enumerate(SHARES):
+        @pl.when(valid(step, 1))
+        def _():
+            share_copies[n].wait_send()
+    for n, step in enumerate(RIMS):
+        @pl.when(valid(step, -1))
+        def _():
+            rim_copies[n].wait_send()
+
+
+def spread_kernel(grown_ref, out_ref):
+    rhs, nx, ny, nz = out_ref.shape
+    side = nx // 4
     for r in range(rhs):
         slices = [
-            grown[at * ny:(at + 1) * ny, r * nz:(r + 1) * nz] for at in range(side + 1)
+            grown_ref[at * ny:(at + 1) * ny, r * nz:(r + 1) * nz] for at in range(side + 1)
         ]
         for x in range(nx):
             at, k = x // 4, x % 4
@@ -487,24 +523,6 @@
                 out_ref[r, x] = slices[at]
             else:
                 out_ref[r, x] = (1 - k / 4) * slices[at] + (k / 4) * slices[at + 1]
-
-    for level in range(3):
-        axis = shift_axis[level]
-
-        @pl.when(me[axis] < peers[axis] - 1)
-        def _():
-            prev_copies[level].wait_send()
-
-        all_slots(scatter_out[level], s_send.at[level], counts[level]).wait()
-        all_slots(gather_in[level], g_send.at[level], counts[level]).wait()
-    for n, step in enumerate(SHARES):
-        @pl.when(valid(step, 1))
-        def _():
-            share_copies[n].wait_send()
-    for n, step in enumerate(RIMS):
-        @pl.when(valid(step, -1))
-        def _():
-            rim_copies[n].wait_send()
 
 
 def per_device(peers, right_side, iterate, coefficient, ordering, leaf_inverse, leaf_first,
@@ -538,9 +556,9 @@
         *[jnp.asarray(m, bf16) for m in mats],
     )
     in_vmem = pl.BlockSpec(memory_space=pltpu.VMEM)
-    return pl.pallas_call(
+    grown = pl.pallas_call(
         functools.partial(kernel, sizes),
-        out_shape=jax.ShapeDtypeStruct(iterate.shape, f32),
+        out_shape=jax.ShapeDtypeStruct(((side + 1) * ny, rhs * nz), f32),
         in_specs=jax.tree.map(lambda _: in_vmem, operands),
         out_specs=in_vmem,
         scratch_shapes=[
@@ -568,8 +586,14 @@
             dma(len(SHARES)), dma(len(SHARES)), dma(3), dma(3), dma(3), dma(3), dma(3), dma(3),
             dma(len(RIMS)), dma(len(RIMS)),
         ],
-        compiler_params=pltpu.CompilerParams(has_side_effects=True),
+        compiler_params=pltpu.CompilerParams(has_side_effects=True, collective_id=0),
     )(*operands)
+    return pl.pallas_call(
+        spread_kernel,
+        out_shape=jax.ShapeDtypeStruct(iterate.shape, f32),
+        in_specs=[in_vmem],
+        out_specs=in_vmem,
+    )(grown)
 
 
 def solution(mesh):

time: 45.5 us -> 42.2 us (0.927)
  local copies, waits for them, and re-layouts: 2.36 us -> 0 us
  Pallas kernels: 43 us -> 42 us
    pallas_call x1, Pallas kernels: 43 us -> 39.8 us  [per_device(): pl.pallas_call(functools.partial(kernel, sizes), out_shape=jax.ShapeDtype...]
    unnamed x1 -> x0, local copies, waits for them, and re-layouts: 2.36 us -> none
    pallas_call x0 -> x1, Pallas kernels: none -> 2.2 us  [per_device(): pl.pallas_call(spread_kernel, out_shape=jax.ShapeDtypeStruct(iterate.shap...]
where the time goes in v3:
time: 42.2 us; the launch traced here: 42 us
  Pallas kernels  42 us (100%)
    pallas_call x1, Pallas kernels, per_device(): pl.pallas_call(functools.partial(kernel, sizes), out_shape=jax.ShapeDtype...  39.8 us
    pallas_call x1, Pallas kernels, per_device(): pl.pallas_call(spread_kernel, out_shape=jax.ShapeDtypeStruct(iterate.shap...  2.2 us

profile of v3, /device:TPU:0, one launch (start us, length us, event | category | flops | bytes accessed | tf_op | source)
XLA Modules:
  0.0 42.0 jit_solution(10307044753061611000)
XLA Ops:
  0.0 39.8 %shard_map.181.grown_ref = f32[168,96]{1,0:T(8,128)} custom-call(f32[4,24,24,24]{3,2,1,0:T(8,128)} %right_ref.1, f32[4,24,24,24]{3,2,1,0:T(8,128)} %u_ref.1, f32[24,24,24]{2,1,0:T(8,128)} %coef_ref.1, s32[1,216]{1,0:T(1,128)} %bitcast.29, f32[125,1,125]{2,1,0:T(1,128)} %bitcast.20, f32[50,1,125]{2,1,0:T(1,128)} %bitcast.24, f32[60,1,125]{2,1,0:T(1,128)} %bitcast.22, ...), custom_call_target="tpu_custom_call" | custom-call | tf_op jit(solution)/shard_map/pallas_call | solution.py:559
  39.8 2.2 %shard_map.182 = f32[4,24,24,24]{3,2,1,0:T(8,128)} custom-call(f32[168,96]{1,0:T(8,128)} %shard_map.181.grown_ref), custom_call_target="tpu_custom_call" | custom-call | tf_op jit(solution)/shard_map/pallas_call | solution.py:591
